TPU v7x, 32 devices: a whole 2x2x4 slice. The times are simulated.
32 devices in a mesh: grp: 1, win: 32 (over z, y, x, core).
Axes of the slice: x: 2, y: 2, z: 4, core: 2. Of those that a mesh axis runs over, the one named last changes fastest.
Arguments:
- tokens: bfloat16 [2, 8, 64, 96, 384], P('grp', None, None, 'win'), may hold values from -6 to 6
- w_upper: bfloat16 [384, 640], replicated, may hold values from -0.3125 to 0.3125
- w_surface: bfloat16 [384, 256], replicated, may hold values from -0.3125 to 0.3125
- bias: float32 [69], replicated, may hold values from -1 to 1
Outputs:
- fields: bfloat16 [2, 17664, 384], P('grp', 'win')
All inputs are finite; a program needn't handle non-finite values.
Results may differ from a plain program's by a relative error of at most 0.0048.
Values may be sent and summed in bfloat16 or wider, within the bound.
A program may use at most 128 MiB of HBM per device.

v0:
```python
import functools

import jax
import jax.numpy as jnp
from jax import lax
from jax.experimental import pallas as pl
from jax.experimental.pallas import tpu as pltpu
from jax.sharding import PartitionSpec as P

VARS_UP = 5
LEVELS = 13
VARS_SF = 4
PATCH = 4
GROUP = 8
CHANNELS = VARS_UP * LEVELS + VARS_SF


def spans_of(owners, own_rows):
    return [
        (o * own_rows // PATCH, -(-(o + 1) * own_rows // PATCH)) for o in range(owners)
    ]


def selector(second, column):
    row = lax.broadcasted_iota(jnp.int32, (128, 128), 0)
    n = lax.broadcasted_iota(jnp.int32, (128, 128), 1)
    step = (n // 16) % 4 - column
    source = (n // 64) * 64 + (((n // 4) % 4 + 2 + 4 * second) % 8) * 8 + n % 4 + 4 * step
    hit = (row == source) & (step >= 0) & (step <= 1)
    return jnp.where(hit, 1.0, 0.0).astype(jnp.bfloat16)


def partner(me, r, windows):
    if windows & (windows - 1):
        return lax.rem(me + r, windows)
    return me ^ r


def kernel(
    plan, tok_hbm, wu_hbm, ws_hbm, bias_ref, out_ref,
    tok_ref, wu_ref, ws_ref, wb_ref, proj_ref, frame_ref, wire_ref, got_ref, place_ref, image_ref,
    load_sem, send_sem, recv_sem,
):
    members, tok_levels, lon_cols, lat_rows, width = tok_ref.shape
    windows, pad_rows, _ = wire_ref.shape
    upper_levels = tok_levels - 1
    up_tiles = wu_ref.shape[1] // 128
    sf_tiles = ws_ref.shape[1] // 128
    me = lax.axis_index("win")

    loads = [
        pltpu.make_async_copy(wu_hbm, wu_ref, load_sem.at[0]),
        pltpu.make_async_copy(ws_hbm, ws_ref, load_sem.at[1]),
        pltpu.make_async_copy(tok_hbm, tok_ref, load_sem.at[2]),
    ]
    for load in loads:
        load.start()

    barrier = pltpu.get_barrier_semaphore()

    def greet(r, carry):
        pl.semaphore_signal(
            barrier, inc=1, device_id={"win": partner(me, r, windows)},
            device_id_type=pl.DeviceIdType.MESH,
        )
        return carry

    lax.fori_loop(1, windows, greet, 0)

    own_rows, low_plan, high_plan = plan
    sel = jnp.concatenate(
        [selector(y, j) for j in range(lon_cols) for y in range(2)], axis=1
    )

    def spread(w):
        wide = jnp.dot(w, sel, preferred_element_type=jnp.float32).astype(jnp.bfloat16)
        for j in range(lon_cols):
            wb_ref[j * width : (j + 1) * width, :] = wide[:, j * 256 : (j + 1) * 256]

    lane = lax.broadcasted_iota(jnp.int32, (lat_rows, 128), 1)
    line = lax.broadcasted_iota(jnp.int32, (lat_rows, 128), 0)
    lower = (lane // 4) % 4 < 2
    low_lanes = lane < 64
    keep = line != jnp.where(lower, 0, lat_rows - 1)

    def image(y):
        first, second = y[:, :128], y[:, 128:]
        moved = jnp.where(
            lower, pltpu.roll(second, 1, 0), pltpu.roll(second, lat_rows - 1, 0)
        )
        return first + jnp.where(keep, moved, 0.0)

    def put(channel, block):
        start = pl.multiple_of(channel * lat_rows, 8)
        frame_ref[pl.ds(start, lat_rows), :] = block

    def multiply(z0, z1):
        rows = (z1 - z0) * lat_rows
        for m in range(members):
            total = None
            for j in range(lon_cols):
                part = jnp.dot(
                    tok_ref[m, z0:z1, j].reshape(rows, width),
                    wb_ref[j * width : (j + 1) * width, :],
                    preferred_element_type=jnp.float32,
                )
                total = part if total is None else total + part
            proj_ref[m, :rows] = total

    def merge(even_channel, odd_channel, i):
        one, two = (
            image(proj_ref[m, i * lat_rows : (i + 1) * lat_rows, :]) for m in range(members)
        )
        put(even_channel, jnp.where(low_lanes, one, pltpu.roll(two, 64, 1)))
        if odd_channel is not None:
            put(odd_channel, jnp.where(low_lanes, pltpu.roll(one, 64, 1), two))

    def copy_to(other):
        return pltpu.make_async_remote_copy(
            src_ref=wire_ref.at[other],
            dst_ref=got_ref.at[me],
            send_sem=send_sem.at[other],
            recv_sem=recv_sem.at[me],
            device_id={"win": other},
            device_id_type=pl.DeviceIdType.MESH,
        )

    def block_of(other):
        start = other * own_rows // PATCH
        return frame_ref[pl.ds(start, pad_rows), :].astype(jnp.bfloat16)

    low = me < windows // 2

    def deliver(slot):
        begin, count, more, extra = (
            jnp.where(low, a, b) for a, b in zip(low_plan[slot], high_plan[slot])
        )
        total = count + extra

        def owner(i):
            i = lax.rem(i + me, jnp.maximum(total, 1))
            return jnp.where(i < count, begin + i, more + i - count)

        def pack(i, carry):
            other = owner(i)
            wire_ref[other] = block_of(other)
            return carry

        def send(i, carry):
            other = owner(i)

            @pl.when(other != me)
            def _():
                copy_to(other).start()

            return carry

        lax.fori_loop(0, total, pack, 0)
        if slot == 0:
            pl.semaphore_wait(barrier, windows - 1)
        lax.fori_loop(0, total, send, 0)

    tail = CHANNELS * lat_rows
    frame_ref[tail:, :] = jnp.zeros((frame_ref.shape[0] - tail, 128), jnp.float32)
    loads[0].wait()
    for slot in range(up_tiles):
        t = jnp.where(low, up_tiles - 1 - slot, slot)
        spread(wu_ref[:, pl.ds(pl.multiple_of(t * 128, 128), 128)])
        if slot == 0:
            loads[1].wait()
            loads[2].wait()
        multiply(0, upper_levels)
        for z in range(upper_levels):
            even = t * LEVELS + 2 * z
            merge(even, even + 1 if 2 * z + 1 < LEVELS else None, z)
        if slot == 1:
            for u in range(sf_tiles):
                spread(ws_ref[:, u * 128 : (u + 1) * 128])
                multiply(upper_levels, tok_levels)
                even = VARS_UP * LEVELS + 2 * u
                merge(even, even + 1, 0)
        deliver(slot)
    got_ref[me] = block_of(me)

    tiles = image_ref.shape[1]
    lons = tiles * 128
    groups = windows // GROUP
    pitch = lons // windows
    row = lax.broadcasted_iota(jnp.int32, (128, GROUP * 128), 0)
    col = lax.broadcasted_iota(jnp.int32, (128, GROUP * 128), 1)
    target = row // 64 * 512 + (row // 4) % 4 * 128 + (row // 16) % 4 * 4 + row % 4

    def fill(i, carry):
        hit = col == target + i * pitch
        place_ref[pl.ds(pl.multiple_of(i * 128, 128), 128), :] = jnp.where(
            hit, 1.0, 0.0
        ).astype(jnp.bfloat16)
        return carry

    lax.fori_loop(0, GROUP, fill, 0)

    def arrived(source):
        pltpu.make_async_remote_copy(
            src_ref=wire_ref.at[source],
            dst_ref=got_ref.at[source],
            send_sem=send_sem.at[source],
            recv_sem=recv_sem.at[source],
            device_id={"win": source},
            device_id_type=pl.DeviceIdType.MESH,
        ).wait_recv()

    def gather(k, carry):
        g = partner(me // GROUP, k, groups)

        def wait_one(i, inner):
            source = g * GROUP + i

            @pl.when(source != me)
            def _():
                arrived(source)

            return inner

        lax.fori_loop(0, GROUP, wait_one, 0)
        stacked = jnp.concatenate([got_ref[g * GROUP + i] for i in range(GROUP)], axis=1)
        moved = jnp.dot(stacked, place_ref[...], preferred_element_type=jnp.float32)
        start = g * (GROUP * pitch) + (lons - PATCH // 2)
        shift = lax.rem(start, 128)
        tile = lax.rem(start // 128, tiles)
        after = lax.rem(tile + 1, tiles)
        first_part = lane_of_pad >= shift
        for m in range(members):
            for q in range(PATCH):
                at = (m * PATCH + q) * 128
                value = pltpu.roll(moved[:, at : at + 128], shift, 1)
                rows = pl.ds(q, pad_rows, stride=PATCH)
                image_ref[m, tile, rows, :] += jnp.where(first_part, value, 0.0)
                image_ref[m, after, rows, :] += jnp.where(first_part, 0.0, value)
        return carry

    lane_of_pad = lax.broadcasted_iota(jnp.int32, (pad_rows, 128), 1)
    image_ref[...] = jnp.zeros(image_ref.shape, jnp.float32)
    lax.fori_loop(0, groups, gather, 0)

    first_row = me * own_rows
    height = lat_rows * PATCH
    row = first_row + lax.broadcasted_iota(jnp.int32, (own_rows, 128), 0)
    first = first_row // height
    last = CHANNELS - 1
    offsets = jnp.zeros((own_rows, 128), jnp.float32)
    for i in range((own_rows - 1) // height + 2):
        channel = jnp.minimum(first + i, last)
        begins = (first + i) * height
        offsets = jnp.where(row >= begins, bias_ref[channel], offsets)
    begin = 0 if own_rows % PATCH == 0 else lax.rem(first_row, PATCH)
    for m in range(members):
        for tile in range(tiles):
            rows = image_ref[m, tile, pl.ds(begin, own_rows), :]
            out_ref[m, :, tile * 128 : (tile + 1) * 128] = (rows + offsets).astype(jnp.bfloat16)

    def sent(r, carry):
        copy_to(partner(me, r, windows)).wait_send()
        return carry

    lax.fori_loop(1, windows, sent, 0)


def write(held_hbm, out_hbm, part_ref, sem):
    members, cuts, _, lanes = part_ref.shape
    pieces = [(m, i) for m in range(members) for i in range(cuts)]

    def view(ref, m, i):
        return ref.at[m, :, i * lanes : (i + 1) * lanes]

    reads = [
        pltpu.make_async_copy(view(held_hbm, m, i), part_ref.at[m, i], sem.at[0, m, i])
        for m, i in pieces
    ]
    writes = [
        pltpu.make_async_copy(part_ref.at[m, i], view(out_hbm, m, i), sem.at[1, m, i])
        for m, i in pieces
    ]
    for read in reads:
        read.start()
    for read, copy in zip(reads, writes):
        read.wait()
        copy.start()
    for copy in writes:
        copy.wait()


def plan_of(spans, lat_rows, tiles):
    owners, depth = len(spans), LEVELS * lat_rows
    surface = tiles * depth
    inner = [o for o in range(owners) if spans[o][1] <= surface]
    low, high = [], []
    done_low, done_high = inner[-1] + 1, 0
    for slot in range(tiles):
        floor = (tiles - 1 - slot) * depth
        begin = min(o for o in range(owners) if spans[o][0] >= floor)
        begin = min(begin, done_low)
        extra = owners - inner[-1] - 1 if slot == 1 else 0
        low.append((begin, done_low - begin, inner[-1] + 1, extra))
        done_low = begin
        ready = sum(1 for lo, hi in spans if hi <= (slot + 1) * depth)
        ready = owners if slot == tiles - 1 else ready
        high.append((done_high, ready - done_high, 0, 0))
        done_high = ready
    return low, high


def body(tokens, w_upper, w_surface, bias):
    members, tok_levels, lat_rows, lon_cols, width = tokens.shape
    windows = lax.axis_size("win")
    own_rows = CHANNELS * lat_rows * PATCH // windows
    lons = windows * lon_cols * PATCH
    spans = spans_of(windows, own_rows)
    pad_rows = -(-max(hi - lo for lo, hi in spans) // 16) * 16
    frame_rows = -(-(spans[-1][0] + pad_rows) // 8) * 8
    low_plan, high_plan = plan_of(spans, lat_rows, w_upper.shape[1] // 128)
    bf16, f32 = jnp.bfloat16, jnp.float32
    by_lon = jnp.transpose(tokens, (0, 1, 3, 2, 4))
    held = pl.pallas_call(
        functools.partial(kernel, (own_rows, low_plan, high_plan)),
        out_shape=jax.ShapeDtypeStruct((members, own_rows, lons), bf16),
        in_specs=[pl.BlockSpec(memory_space=pltpu.HBM)] * 3
        + [pl.BlockSpec(memory_space=pltpu.SMEM)],
        out_specs=pl.BlockSpec(memory_space=pltpu.VMEM),
        scratch_shapes=[
            pltpu.VMEM(by_lon.shape, bf16),
            pltpu.VMEM(w_upper.shape, bf16),
            pltpu.VMEM(w_surface.shape, bf16),
            pltpu.VMEM((lon_cols * width, 256), bf16),
            pltpu.VMEM((members, (tok_levels - 1) * lat_rows, 256), f32),
            pltpu.VMEM((frame_rows, 128), f32),
            pltpu.VMEM((windows, pad_rows, 128), bf16),
            pltpu.VMEM((windows, pad_rows, 128), bf16),
            pltpu.VMEM((GROUP * 128, GROUP * 128), bf16),
            pltpu.VMEM((members, lons // 128, pad_rows * PATCH, 128), f32),
            pltpu.SemaphoreType.DMA((3,)),
            pltpu.SemaphoreType.DMA((windows,)),
            pltpu.SemaphoreType.DMA((windows,)),
        ],
        compiler_params=pltpu.CompilerParams(
            collective_id=0, has_side_effects=True, vmem_limit_bytes=65 * 1000 * 1000
        ),
    )(by_lon, w_upper, w_surface, bias)
    return pl.pallas_call(
        write,
        out_shape=jax.ShapeDtypeStruct((members, own_rows, lons), bf16),
        in_specs=[pl.BlockSpec(memory_space=pl.ANY)],
        out_specs=pl.BlockSpec(memory_space=pl.ANY),
        scratch_shapes=[
            pltpu.VMEM((members, 3, own_rows, lons // 3), bf16),
            pltpu.SemaphoreType.DMA((2, members, 3)),
        ],
    )(held)


def solution(mesh):
    placed = (P("grp", None, None, "win", None), P(), P(), P())
    return jax.shard_map(
        body, mesh=mesh, in_specs=placed, out_specs=P("grp", "win", None), check_vma=False
    )
```

profile of v0, /device:TPU:15, one launch (start us, length us, event | category | flops | bytes accessed | tf_op | source)
XLA Modules:
  0.0 37.3 jit_solution(17756726793564838321)
XLA Ops:
  0.0 35.3 %shard_map.46.held_hbm = bf16[2,552,384]{2,1,0:T(8,128)(2,1)} custom-call(bf16[2,8,3,64,384]{4,3,2,1,0:T(8,128)(2,1)} %bitcast.1, bf16[384,640]{1,0:T(8,128)(2,1)} %wu_hbm.1, bf16[384,256]{1,0:T(8,128)(2,1)} %ws_hbm.1, f32[69]{0:T(128)} %bias_ref.1), custom_call_target="tpu_custom_call" | custom-call | tf_op jit(solution)/shard_map/pallas_call | solution.py:323
  35.3 2.0 %shard_map.47 = bf16[2,552,384]{2,1,0:T(8,128)(2,1)} custom-call(bf16[2,552,384]{2,1,0:T(8,128)(2,1)} %shard_map.46.held_hbm), custom_call_target="tpu_custom_call" | custom-call | tf_op jit(solution)/shard_map/pallas_call | solution.py:348
where the time goes:
time: 37.5 us; the launch traced here: 37.3 us
  Pallas kernels  37.3 us (99%)
    pallas_call x1, Pallas kernels, body(): pl.pallas_call(functools.partial(kernel, (own_rows, low_plan, high_plan))...  35.3 us
    pallas_call x1, Pallas kernels, body(): pl.pallas_call(write, out_shape=jax.ShapeDtypeStruct((members, own_rows,...  2 us

commit v1 on v0

--- a/solution.py
+++ b/solution.py
@@ -265,30 +265,6 @@
     lax.fori_loop(1, windows, sent, 0)
 
 
-def write(held_hbm, out_hbm, part_ref, sem):
-    members, cuts, _, lanes = part_ref.shape
-    pieces = [(m, i) for m in range(members) for i in range(cuts)]
-
-    def view(ref, m, i):
-        return ref.at[m, :, i * lanes : (i + 1) * lanes]
-
-    reads = [
-        pltpu.make_async_copy(view(held_hbm, m, i), part_ref.at[m, i], sem.at[0, m, i])
-        for m, i in pieces
-    ]
-    writes = [
-        pltpu.make_async_copy(part_ref.at[m, i], view(out_hbm, m, i), sem.at[1, m, i])
-        for m, i in pieces
-    ]
-    for read in reads:
-        read.start()
-    for read, copy in zip(reads, writes):
-        read.wait()
-        copy.start()
-    for copy in writes:
-        copy.wait()
-
-
 def plan_of(spans, lat_rows, tiles):
     owners, depth = len(spans), LEVELS * lat_rows
     surface = tiles * depth
@@ -320,9 +296,9 @@
     low_plan, high_plan = plan_of(spans, lat_rows, w_upper.shape[1] // 128)
     bf16, f32 = jnp.bfloat16, jnp.float32
     by_lon = jnp.transpose(tokens, (0, 1, 3, 2, 4))
-    held = pl.pallas_call(
+    return pl.pallas_call(
         functools.partial(kernel, (own_rows, low_plan, high_plan)),
-        out_shape=jax.ShapeDtypeStruct((members, own_rows, lons), bf16),
+        out_shape=pltpu.VMEM((members, own_rows, lons), bf16),
         in_specs=[pl.BlockSpec(memory_space=pltpu.HBM)] * 3
         + [pl.BlockSpec(memory_space=pltpu.SMEM)],
         out_specs=pl.BlockSpec(memory_space=pltpu.VMEM),
@@ -345,16 +321,6 @@
             collective_id=0, has_side_effects=True, vmem_limit_bytes=65 * 1000 * 1000
         ),
     )(by_lon, w_upper, w_surface, bias)
-    return pl.pallas_call(
-        write,
-        out_shape=jax.ShapeDtypeStruct((members, own_rows, lons), bf16),
-        in_specs=[pl.BlockSpec(memory_space=pl.ANY)],
-        out_specs=pl.BlockSpec(memory_space=pl.ANY),
-        scratch_shapes=[
-            pltpu.VMEM((members, 3, own_rows, lons // 3), bf16),
-            pltpu.SemaphoreType.DMA((2, members, 3)),
-        ],
-    )(held)
 
 
 def solution(mesh):

time: 37.5 us -> 35.4 us (0.944)
  Pallas kernels: 37.3 us -> 34.4 us
  local copies, waits for them, and re-layouts: 0 us -> 0.9 us
    pallas_call x1 -> x0, Pallas kernels: 2 us -> none  [body(): pl.pallas_call(write, out_shape=jax.ShapeDtypeStruct((members, own_rows,...]
    pallas_call x1, Pallas kernels: 35.3 us -> 34.4 us  [body(): pl.pallas_call(functools.partial(kernel, (own_rows, low_plan, high_plan))...]
    unnamed x0 -> x1, local copies, waits for them, and re-layouts: none -> 0.9 us
where the time goes in v1:
time: 35.4 us; the launch traced here: 35.3 us
  Pallas kernels  34.4 us (97%)
  local copies, waits for them, and re-layouts  0.9 us (3%)
    pallas_call x1, Pallas kernels, body(): pl.pallas_call(functools.partial(kernel, (own_rows, low_plan, high_plan))...  34.4 us
    unnamed x1, local copies, waits for them, and re-layouts  0.9 us

profile of v1, /device:TPU:15, one launch (start us, length us, event | category | flops | bytes accessed | tf_op | source)
XLA Modules:
  0.0 35.3 jit_solution(7753036758167011460)
XLA Ops:
  0.0 34.4 %shard_map.46 = bf16[2,552,384]{2,1,0:T(8,128)(2,1)S(1)} custom-call(bf16[2,8,3,64,384]{4,3,2,1,0:T(8,128)(2,1)} %bitcast.1, bf16[384,640]{1,0:T(8,128)(2,1)} %wu_hbm.1, bf16[384,256]{1,0:T(8,128)(2,1)} %ws_hbm.1, f32[69]{0:T(128)} %bias_ref.1), custom_call_target="tpu_custom_call" | custom-call | tf_op jit(solution)/shard_map/pallas_call | solution.py:299
  34.4 0.9 %copy.6 = bf16[2,552,384]{2,1,0:T(8,128)(2,1)} copy(bf16[2,552,384]{2,1,0:T(8,128)(2,1)S(1)} %shard_map.46) | data formatting | bytes 1695744

commit v2 on v1

--- a/solution.py
+++ b/solution.py
@@ -21,12 +21,21 @@
     ]
 
 
-def selector(second, column):
+def place_of(lane):
+    u = lane % 64
+    own = u < 48
+    q = jnp.where(own, jnp.where(u >= 24, 2, 0) + jnp.where(u % 24 >= 12, 1, 0), (u - 48) // 4)
+    column = jnp.where(own, u - 12 * q, 12 + u % 4)
+    return q, column, own
+
+
+def selector(second, token):
     row = lax.broadcasted_iota(jnp.int32, (128, 128), 0)
     n = lax.broadcasted_iota(jnp.int32, (128, 128), 1)
-    step = (n // 16) % 4 - column
-    source = (n // 64) * 64 + (((n // 4) % 4 + 2 + 4 * second) % 8) * 8 + n % 4 + 4 * step
-    hit = (row == source) & (step >= 0) & (step <= 1)
+    q, column, _ = place_of(n)
+    k = column - PATCH * token
+    source = n // 64 * 64 + (q + 2 + 4 * second) % 8 * 8 + k
+    hit = (row == source) & (k >= 0) & (k < 2 * PATCH)
     return jnp.where(hit, 1.0, 0.0).astype(jnp.bfloat16)
 
 
@@ -38,15 +47,18 @@
 
 def kernel(
     plan, tok_hbm, wu_hbm, ws_hbm, bias_ref, out_ref,
-    tok_ref, wu_ref, ws_ref, wb_ref, proj_ref, frame_ref, wire_ref, got_ref, place_ref, image_ref,
-    load_sem, send_sem, recv_sem,
+    tok_ref, wu_ref, ws_ref, wb_ref, proj_ref, frame_ref, wire_ref, got_ref, edge_ref, side_ref, spot_ref,
+    place_ref, image_ref, load_sem, send_sem, recv_sem, edge_sem,
 ):
     members, tok_levels, lon_cols, lat_rows, width = tok_ref.shape
     windows, pad_rows, _ = wire_ref.shape
+    half = windows // 2
     upper_levels = tok_levels - 1
     up_tiles = wu_ref.shape[1] // 128
     sf_tiles = ws_ref.shape[1] // 128
     me = lax.axis_index("win")
+    own_rows, main_rows, low_plan, high_plan = plan
+    tail_rows = pad_rows - main_rows
 
     loads = [
         pltpu.make_async_copy(wu_hbm, wu_ref, load_sem.at[0]),
@@ -67,7 +79,6 @@
 
     lax.fori_loop(1, windows, greet, 0)
 
-    own_rows, low_plan, high_plan = plan
     sel = jnp.concatenate(
         [selector(y, j) for j in range(lon_cols) for y in range(2)], axis=1
     )
@@ -79,9 +90,16 @@
 
     lane = lax.broadcasted_iota(jnp.int32, (lat_rows, 128), 1)
     line = lax.broadcasted_iota(jnp.int32, (lat_rows, 128), 0)
-    lower = (lane // 4) % 4 < 2
+    lane_q, _, own_lane = place_of(lane)
+    lower = lane_q < 2
     low_lanes = lane < 64
     keep = line != jnp.where(lower, 0, lat_rows - 1)
+
+    def own_lanes(rows):
+        return lax.broadcasted_iota(jnp.int32, (rows, 128), 1) % 64 < 48
+
+    def chunk_lanes(rows, c):
+        return lax.broadcasted_iota(jnp.int32, (rows, 128), 1) % 64 // 16 == c
 
     def image(y):
         first, second = y[:, :128], y[:, 128:]
@@ -92,7 +110,7 @@
 
     def put(channel, block):
         start = pl.multiple_of(channel * lat_rows, 8)
-        frame_ref[pl.ds(start, lat_rows), :] = block
+        frame_ref[pl.ds(start, lat_rows), :] = block + jnp.where(own_lane, bias_ref[channel], 0.0)
 
     def multiply(z0, z1):
         rows = (z1 - z0) * lat_rows
@@ -115,21 +133,81 @@
         if odd_channel is not None:
             put(odd_channel, jnp.where(low_lanes, pltpu.roll(one, 64, 1), two))
 
-    def copy_to(other):
+    left_open = lax.rem(me, half) == 0
+    right_open = lax.rem(me + 1, half) == 0
+
+    def edge_copy(index, rows):
         return pltpu.make_async_remote_copy(
-            src_ref=wire_ref.at[other],
-            dst_ref=got_ref.at[me],
+            src_ref=edge_ref.at[index, 0:rows],
+            dst_ref=side_ref.at[index, 0:rows],
+            send_sem=edge_sem.at[0, index],
+            recv_sem=edge_sem.at[1, index],
+            device_id={"win": lax.rem(me + 1, windows)},
+            device_id_type=pl.DeviceIdType.MESH,
+        )
+
+    def give_edge(index, base, count):
+        rows = count // 4
+        packed = frame_ref[pl.ds(pl.multiple_of(base + 3 * rows, 8), rows), :]
+        for c in range(3):
+            part = frame_ref[pl.ds(pl.multiple_of(base + c * rows, 8), rows), :]
+            packed = jnp.where(chunk_lanes(rows, c), pltpu.roll(part, 80 + 16 * c, 1), packed)
+        edge_ref[index, 0:rows] = packed.astype(jnp.bfloat16)
+
+    def send_edge(index, count):
+        @pl.when(jnp.logical_not(right_open))
+        def _():
+            edge_copy(index, count // 4).start()
+
+    def take_edge(index, base, count):
+        rows = count // 4
+
+        @pl.when(jnp.logical_not(left_open))
+        def _():
+            edge_copy(index, rows).wait_recv()
+            moved = jnp.dot(
+                side_ref[index, 0:rows], spot_ref[...], preferred_element_type=jnp.float32
+            )
+            for c in range(4):
+                at = pl.ds(pl.multiple_of(base + c * rows, 8), rows)
+                frame_ref[at, :] += moved[:, c * 128 : (c + 1) * 128]
+
+    def rows_of(window):
+        return lax.rem(window + 1, half) == 0
+
+    def copy_of(source, other, rows):
+        return pltpu.make_async_remote_copy(
+            src_ref=wire_ref.at[other, 0:rows],
+            dst_ref=got_ref.at[source, 0:rows],
             send_sem=send_sem.at[other],
-            recv_sem=recv_sem.at[me],
+            recv_sem=recv_sem.at[source],
             device_id={"win": other},
             device_id_type=pl.DeviceIdType.MESH,
         )
 
-    def block_of(other):
+    def either(is_open, run):
+        @pl.when(is_open)
+        def _():
+            run(pad_rows)
+
+        @pl.when(jnp.logical_not(is_open))
+        def _():
+            run(main_rows)
+
+    def pack_into(ref, index, other):
         start = other * own_rows // PATCH
-        return frame_ref[pl.ds(start, pad_rows), :].astype(jnp.bfloat16)
-
-    low = me < windows // 2
+        main = frame_ref[pl.ds(start, main_rows), :]
+        tail = frame_ref[pl.ds(start + main_rows, tail_rows), :]
+        parts = [pltpu.roll(tail, 48 - 16 * c, 1) for c in range(3)]
+        if main_rows > 3 * tail_rows:
+            parts.append(main[3 * tail_rows :])
+        kept = own_lanes(main_rows) | right_open
+        ref[index, 0:main_rows] = jnp.where(kept, main, jnp.concatenate(parts, axis=0)).astype(
+            jnp.bfloat16
+        )
+        ref[index, main_rows:pad_rows] = tail.astype(jnp.bfloat16)
+
+    low = me < half
 
     def deliver(slot):
         begin, count, more, extra = (
@@ -141,30 +219,47 @@
             i = lax.rem(i + me, jnp.maximum(total, 1))
             return jnp.where(i < count, begin + i, more + i - count)
 
-        def pack(i, carry):
-            other = owner(i)
-            wire_ref[other] = block_of(other)
-            return carry
-
         def send(i, carry):
             other = owner(i)
 
             @pl.when(other != me)
             def _():
-                copy_to(other).start()
+                pack_into(wire_ref, other, other)
+                either(right_open, lambda rows: copy_of(me, other, rows).start())
 
             return carry
 
-        lax.fori_loop(0, total, pack, 0)
-        if slot == 0:
-            pl.semaphore_wait(barrier, windows - 1)
         lax.fori_loop(0, total, send, 0)
 
-    tail = CHANNELS * lat_rows
-    frame_ref[tail:, :] = jnp.zeros((frame_ref.shape[0] - tail, 128), jnp.float32)
+    def clear(i, carry):
+        frame_ref[pl.ds(pl.multiple_of(i * 8, 8), 8), :] = jnp.zeros((8, 128), jnp.float32)
+        return carry
+
+    lax.fori_loop(0, frame_ref.shape[0] // 8, clear, 0)
+    from_row = lax.broadcasted_iota(jnp.int32, spot_ref.shape, 0)
+    to_col = lax.broadcasted_iota(jnp.int32, spot_ref.shape, 1)
+    to_lane = from_row // 64 * 64 + from_row % 16 // 4 * 12 + from_row % 4
+    spot_ref[...] = jnp.where(
+        to_col == from_row % 64 // 16 * 128 + to_lane, 1.0, 0.0
+    ).astype(jnp.bfloat16)
+
+    depth = LEVELS * lat_rows
+    surface = VARS_UP * depth
+    shallow = VARS_SF * lat_rows
+
+    def base_of(slot):
+        t = jnp.where(low, up_tiles - 1 - slot, slot)
+        return t, t * depth
+
+    def settle(slot):
+        take_edge(slot, base_of(slot)[1], depth)
+        if slot == 1:
+            take_edge(up_tiles, surface, shallow)
+        deliver(slot)
+
     loads[0].wait()
     for slot in range(up_tiles):
-        t = jnp.where(low, up_tiles - 1 - slot, slot)
+        t, base = base_of(slot)
         spread(wu_ref[:, pl.ds(pl.multiple_of(t * 128, 128), 128)])
         if slot == 0:
             loads[1].wait()
@@ -173,14 +268,22 @@
         for z in range(upper_levels):
             even = t * LEVELS + 2 * z
             merge(even, even + 1 if 2 * z + 1 < LEVELS else None, z)
+        give_edge(slot, base, depth)
+        if slot == 0:
+            pl.semaphore_wait(barrier, windows - 1)
+        send_edge(slot, depth)
         if slot == 1:
             for u in range(sf_tiles):
                 spread(ws_ref[:, u * 128 : (u + 1) * 128])
                 multiply(upper_levels, tok_levels)
                 even = VARS_UP * LEVELS + 2 * u
                 merge(even, even + 1, 0)
-        deliver(slot)
-    got_ref[me] = block_of(me)
+            give_edge(up_tiles, surface, shallow)
+            send_edge(up_tiles, shallow)
+        if slot > 0:
+            settle(slot - 1)
+    settle(up_tiles - 1)
+    pack_into(got_ref, me, me)
 
     tiles = image_ref.shape[1]
     lons = tiles * 128
@@ -188,10 +291,11 @@
     pitch = lons // windows
     row = lax.broadcasted_iota(jnp.int32, (128, GROUP * 128), 0)
     col = lax.broadcasted_iota(jnp.int32, (128, GROUP * 128), 1)
-    target = row // 64 * 512 + (row // 4) % 4 * 128 + (row // 16) % 4 * 4 + row % 4
+    row_q, row_column, row_own = place_of(row)
+    target = row // 64 * 512 + row_q * 128 + row_column
 
     def fill(i, carry):
-        hit = col == target + i * pitch
+        hit = (col == target + i * pitch) & (row_own | (i == GROUP - 1))
         place_ref[pl.ds(pl.multiple_of(i * 128, 128), 128), :] = jnp.where(
             hit, 1.0, 0.0
         ).astype(jnp.bfloat16)
@@ -199,15 +303,20 @@
 
     lax.fori_loop(0, GROUP, fill, 0)
 
-    def arrived(source):
-        pltpu.make_async_remote_copy(
-            src_ref=wire_ref.at[source],
-            dst_ref=got_ref.at[source],
-            send_sem=send_sem.at[source],
-            recv_sem=recv_sem.at[source],
-            device_id={"win": source},
-            device_id_type=pl.DeviceIdType.MESH,
-        ).wait_recv()
+    def unpack(source, may_be_open):
+        main = got_ref[source, 0:main_rows]
+        tail = jnp.zeros((tail_rows, 128), jnp.float32)
+        for c in range(3):
+            part = got_ref[source, c * tail_rows : (c + 1) * tail_rows].astype(jnp.float32)
+            part = pltpu.roll(part, 80 + 16 * c, 1)
+            tail = jnp.where(chunk_lanes(tail_rows, c), part, tail)
+        if may_be_open:
+            is_open = rows_of(source)
+            raw = got_ref[source, main_rows:pad_rows].astype(jnp.float32)
+            tail = jnp.where(is_open, raw, tail)
+            wide = jnp.where(own_lanes(main_rows) | is_open, main.astype(jnp.float32), 0.0)
+            main = wide.astype(jnp.bfloat16)
+        return jnp.concatenate([main, tail.astype(jnp.bfloat16)], axis=0)
 
     def gather(k, carry):
         g = partner(me // GROUP, k, groups)
@@ -217,12 +326,14 @@
 
             @pl.when(source != me)
             def _():
-                arrived(source)
+                either(rows_of(source), lambda rows: copy_of(source, source, rows).wait_recv())
 
             return inner
 
         lax.fori_loop(0, GROUP, wait_one, 0)
-        stacked = jnp.concatenate([got_ref[g * GROUP + i] for i in range(GROUP)], axis=1)
+        stacked = jnp.concatenate(
+            [unpack(g * GROUP + i, i == GROUP - 1) for i in range(GROUP)], axis=1
+        )
         moved = jnp.dot(stacked, place_ref[...], preferred_element_type=jnp.float32)
         start = g * (GROUP * pitch) + (lons - PATCH // 2)
         shift = lax.rem(start, 128)
@@ -242,27 +353,33 @@
     image_ref[...] = jnp.zeros(image_ref.shape, jnp.float32)
     lax.fori_loop(0, groups, gather, 0)
 
-    first_row = me * own_rows
-    height = lat_rows * PATCH
-    row = first_row + lax.broadcasted_iota(jnp.int32, (own_rows, 128), 0)
-    first = first_row // height
-    last = CHANNELS - 1
-    offsets = jnp.zeros((own_rows, 128), jnp.float32)
-    for i in range((own_rows - 1) // height + 2):
-        channel = jnp.minimum(first + i, last)
-        begins = (first + i) * height
-        offsets = jnp.where(row >= begins, bias_ref[channel], offsets)
-    begin = 0 if own_rows % PATCH == 0 else lax.rem(first_row, PATCH)
+    begin = 0 if own_rows % PATCH == 0 else lax.rem(me * own_rows, PATCH)
     for m in range(members):
         for tile in range(tiles):
             rows = image_ref[m, tile, pl.ds(begin, own_rows), :]
-            out_ref[m, :, tile * 128 : (tile + 1) * 128] = (rows + offsets).astype(jnp.bfloat16)
+            out_ref[m, :, tile * 128 : (tile + 1) * 128] = rows.astype(jnp.bfloat16)
 
     def sent(r, carry):
-        copy_to(partner(me, r, windows)).wait_send()
+        other = partner(me, r, windows)
+        either(right_open, lambda rows: copy_of(me, other, rows).wait_send())
         return carry
 
     lax.fori_loop(1, windows, sent, 0)
+
+    @pl.when(jnp.logical_not(right_open))
+    def _():
+        for index in range(up_tiles):
+            edge_copy(index, depth // 4).wait_send()
+        edge_copy(up_tiles, shallow // 4).wait_send()
+
+
+def rows_for(longest):
+    main = 16
+    while True:
+        tail = max(16, -(-(longest - main) // 16) * 16)
+        if 3 * tail <= main:
+            return main, tail
+        main += 16
 
 
 def plan_of(spans, lat_rows, tiles):
@@ -291,13 +408,15 @@
     own_rows = CHANNELS * lat_rows * PATCH // windows
     lons = windows * lon_cols * PATCH
     spans = spans_of(windows, own_rows)
-    pad_rows = -(-max(hi - lo for lo, hi in spans) // 16) * 16
+    main_rows, tail_rows = rows_for(max(hi - lo for lo, hi in spans))
+    pad_rows = main_rows + tail_rows
     frame_rows = -(-(spans[-1][0] + pad_rows) // 8) * 8
     low_plan, high_plan = plan_of(spans, lat_rows, w_upper.shape[1] // 128)
+    edges = w_upper.shape[1] // 128 + 1
     bf16, f32 = jnp.bfloat16, jnp.float32
     by_lon = jnp.transpose(tokens, (0, 1, 3, 2, 4))
     return pl.pallas_call(
-        functools.partial(kernel, (own_rows, low_plan, high_plan)),
+        functools.partial(kernel, (own_rows, main_rows, low_plan, high_plan)),
         out_shape=pltpu.VMEM((members, own_rows, lons), bf16),
         in_specs=[pl.BlockSpec(memory_space=pltpu.HBM)] * 3
         + [pl.BlockSpec(memory_space=pltpu.SMEM)],
@@ -311,11 +430,15 @@
             pltpu.VMEM((frame_rows, 128), f32),
             pltpu.VMEM((windows, pad_rows, 128), bf16),
             pltpu.VMEM((windows, pad_rows, 128), bf16),
+            pltpu.VMEM((edges, LEVELS * lat_rows // 4, 128), bf16),
+            pltpu.VMEM((edges, LEVELS * lat_rows // 4, 128), bf16),
+            pltpu.VMEM((128, 4 * 128), bf16),
             pltpu.VMEM((GROUP * 128, GROUP * 128), bf16),
             pltpu.VMEM((members, lons // 128, pad_rows * PATCH, 128), f32),
             pltpu.SemaphoreType.DMA((3,)),
             pltpu.SemaphoreType.DMA((windows,)),
             pltpu.SemaphoreType.DMA((windows,)),
+            pltpu.SemaphoreType.DMA((2, edges)),
         ],
         compiler_params=pltpu.CompilerParams(
             collective_id=0, has_side_effects=True, vmem_limit_bytes=65 * 1000 * 1000

time: 35.4 us -> 37.2 us (1.051)
  the two profiles are of different devices: /device:TPU:15 before, /device:TPU:0 now
where the time goes in v2:
time: 37.2 us; the launch traced here: 37 us
  Pallas kernels  36.1 us (97%)
  local copies, waits for them, and re-layouts  0.9 us (2%)
    pallas_call x1, Pallas kernels, body(): pl.pallas_call(functools.partial(kernel, (own_rows, main_rows, low_plan,...  36.1 us
    unnamed x1, local copies, waits for them, and re-layouts  0.9 us

profile of v2, /device:TPU:0, one launch (start us, length us, event | category | flops | bytes accessed | tf_op | source)
XLA Modules:
  0.0 37.0 jit_solution(14537039168956678874)
XLA Ops:
  0.0 36.1 %shard_map.46 = bf16[2,552,384]{2,1,0:T(8,128)(2,1)S(1)} custom-call(bf16[2,8,3,64,384]{4,3,2,1,0:T(8,128)(2,1)} %bitcast.1, bf16[384,640]{1,0:T(8,128)(2,1)} %wu_hbm.1, bf16[384,256]{1,0:T(8,128)(2,1)} %ws_hbm.1, f32[69]{0:T(128)} %bias_ref.1), custom_call_target="tpu_custom_call" | custom-call | tf_op jit(solution)/shard_map/pallas_call | solution.py:418
  36.1 0.9 %copy.6 = bf16[2,552,384]{2,1,0:T(8,128)(2,1)} copy(bf16[2,552,384]{2,1,0:T(8,128)(2,1)S(1)} %shard_map.46) | data formatting | bytes 1695744

commit v3 on v2

v3 whole, which is shorter than its diff:
```python
import functools

import jax
import jax.numpy as jnp
from jax import lax
from jax.experimental import pallas as pl
from jax.experimental.pallas import tpu as pltpu
from jax.sharding import PartitionSpec as P

VARS_UP = 5
LEVELS = 13
VARS_SF = 4
PATCH = 4
GROUP = 8
TO_SPARE = (36, 32, 4)
CHANNELS = VARS_UP * LEVELS + VARS_SF


def spans_of(owners, own_rows):
    return [
        (o * own_rows // PATCH, -(-(o + 1) * own_rows // PATCH)) for o in range(owners)
    ]


def place_of(lane):
    return lane // 8 % 4, lane // 32 % 2 * 8 + lane % 8


def partner(me, r, windows):
    if windows & (windows - 1):
        return lax.rem(me + r, windows)
    return me ^ r


def kernel(
    plan, tok_hbm, wu_hbm, ws_hbm, bias_ref, out_ref,
    tok_ref, wu_ref, ws_ref, wb_ref, proj_ref, frame_ref, wire_ref, got_ref, edge_ref, side_ref, spot_ref,
    sel_ref, pick_ref,    place_ref, image_ref, load_sem, send_sem, recv_sem, edge_sem,
):
    members, tok_levels, lon_cols, lat_rows, width = tok_ref.shape
    windows, pad_rows, _ = wire_ref.shape
    half = windows // 2
    upper_levels = tok_levels - 1
    up_tiles = wu_ref.shape[1] // 128
    sf_tiles = ws_ref.shape[1] // 128
    me = lax.axis_index("win")
    own_rows, main_rows, low_plan, high_plan = plan
    tail_rows = pad_rows - main_rows

    last = lon_cols - 1
    loads = [
        pltpu.make_async_copy(wu_hbm, wu_ref, load_sem.at[0]),
        pltpu.make_async_copy(ws_hbm, ws_ref, load_sem.at[1]),
        pltpu.make_async_copy(tok_hbm.at[:, :, last], tok_ref.at[:, :, last], load_sem.at[2]),
        pltpu.make_async_copy(
            tok_hbm.at[:, :, 0:last], tok_ref.at[:, :, 0:last], load_sem.at[3]
        ),
    ]
    for load in loads:
        load.start()

    barrier = pltpu.get_barrier_semaphore()

    def greet(r, carry):
        pl.semaphore_signal(
            barrier, inc=1, device_id={"win": partner(me, r, windows)},
            device_id_type=pl.DeviceIdType.MESH,
        )
        return carry

    lax.fori_loop(1, windows, greet, 0)

    def iota(shape, axis):
        return lax.broadcasted_iota(jnp.int32, shape, axis)

    def one_hot(hit):
        return jnp.where(hit, 1.0, 0.0).astype(jnp.bfloat16)

    def second_of(lat, half):
        return (lat + 2 + 4 * half) % 8

    def source_of(tile, level, lat, lon):
        return tile * 128 + level * 64 + lat * 8 + lon

    for side in range(2):
        for near in range(2):
            row = iota((256, 256), 0)
            n = iota((256, 256), 1)
            k = side * 8 + n % 8 - PATCH * (side + near)
            lat = second_of(n // 8 % 4, n // 128)
            hit = row == source_of(n // 64 % 2, n // 32 % 2, lat, k)
            at = (2 * side + near) * 256
            sel_ref[:, at : at + 256] = one_hot(hit & (k >= 0) & (k < 2 * PATCH))
    row = iota(pick_ref.shape, 0)
    n = iota(pick_ref.shape, 1)
    lat = second_of(n // 4 % 4, n // 128)
    pick_ref[...] = one_hot(row == source_of(n // 32 % 4, n // 16 % 2, lat, n % 4 + PATCH))
    row = iota(spot_ref.shape, 0)
    n = iota(spot_ref.shape, 1)
    to_lane = row // 64 * 64 + row // 4 % 4 * 8 + row % 4
    spot_ref[...] = one_hot(n == row // 16 % 4 * 128 + to_lane)

    def spread(w):
        wide = jnp.dot(w, sel_ref[0 : w.shape[1], :], preferred_element_type=jnp.float32)
        for side in range(2):
            for near in range(2):
                at = (2 * side + near) * 256
                wb_ref[side, near * width : (near + 1) * width, :] = wide[
                    :, at : at + 256
                ].astype(jnp.bfloat16)

    lane = iota((lat_rows, 128), 1)
    line = iota((lat_rows, 128), 0)
    frame_lower = lane % 32 < 16
    edge_lower = lane % 16 < 8
    own_lane = place_of(lane)[1] < 12

    def own_lanes(rows):
        return place_of(iota((rows, 128), 1))[1] < 12

    def chunk_lanes(rows, c):
        return place_of(iota((rows, 128), 1))[1] // 4 == c

    def image(y, lower):
        first, second = y[:, :128], y[:, 128:]
        moved = jnp.where(
            lower, pltpu.roll(second, 1, 0), pltpu.roll(second, lat_rows - 1, 0)
        )
        keep = line != jnp.where(lower, 0, lat_rows - 1)
        return first + jnp.where(keep, moved, 0.0)

    def exchange(parts, wanted):
        at = iota(parts[0].shape, 1)
        low_half, even = at < 64, at // 32 % 2 == 0
        halves = []
        for h in range(-(-wanted // 2)):
            for a, b in ((parts[0], parts[2]), (parts[1], parts[3])):
                if h == 0:
                    halves.append(jnp.where(low_half, a, pltpu.roll(b, 64, 1)))
                else:
                    halves.append(jnp.where(low_half, pltpu.roll(a, 64, 1), b))
        out = []
        for p in range(wanted):
            a, b = halves[p // 2 * 2], halves[p // 2 * 2 + 1]
            if p % 2 == 0:
                out.append(jnp.where(even, a, pltpu.roll(b, 32, 1)))
            else:
                out.append(jnp.where(even, pltpu.roll(a, 96, 1), b))
        return out

    def put(channel, block):
        start = pl.multiple_of(channel * lat_rows, 8)
        frame_ref[pl.ds(start, lat_rows), :] = block + jnp.where(own_lane, bias_ref[channel], 0.0)

    def multiply(z0, z1):
        rows = (z1 - z0) * lat_rows
        for m in range(members):
            token = [tok_ref[m, z0:z1, j].reshape(rows, width) for j in range(lon_cols)]
            for side in range(2):
                proj_ref[m, side, 0:rows] = jnp.dot(
                    jnp.concatenate(token[side : side + 2], axis=1), wb_ref[side],
                    preferred_element_type=jnp.float32,
                )

    def merge(z, channels):
        at = slice(z * lat_rows, (z + 1) * lat_rows)
        parts = [
            image(proj_ref[m, side, at, :], frame_lower)
            for m in range(members)
            for side in range(2)
        ]
        for channel, block in zip(channels, exchange(parts, len(channels))):
            if channel is not None:
                put(channel, block)

    low = me < half

    def first_tile(slot):
        return jnp.where(low, max(up_tiles - 2 * (slot + 1), 0), 2 * slot)

    def tiles_of(slot):
        return min(2, up_tiles - 2 * slot)

    left_open = lax.rem(me, half) == 0
    right_open = lax.rem(me + 1, half) == 0

    def edge_copy(index, rows):
        return pltpu.make_async_remote_copy(
            src_ref=edge_ref.at[index, 0:rows],
            dst_ref=side_ref.at[index, 0:rows],
            send_sem=edge_sem.at[0, index],
            recv_sem=edge_sem.at[1, index],
            device_id={"win": lax.rem(me + 1, windows)},
            device_id_type=pl.DeviceIdType.MESH,
        )

    part_rows = lat_rows // 2
    edge_rows = upper_levels * part_rows

    def edges(w, z0, z1, put_edge):
        rows = (z1 - z0) * lat_rows
        weights = jnp.dot(w, pick_ref[0 : w.shape[1], :], preferred_element_type=jnp.float32)
        weights = weights.astype(jnp.bfloat16)
        for m in range(members):
            proj_ref[m, 0, 0:rows] = jnp.dot(
                tok_ref[m, z0:z1, last].reshape(rows, width), weights,
                preferred_element_type=jnp.float32,
            )
        for z in range(z1 - z0):
            parts = []
            for m in range(members):
                x = image(proj_ref[m, 0, z * lat_rows : (z + 1) * lat_rows, :], edge_lower)
                parts += [x[:part_rows], x[part_rows:]]
            for i, block in enumerate(exchange(parts, w.shape[1] // 128)):
                put_edge(i, z, block.astype(jnp.bfloat16))

    def make_edges():
        loads[0].wait()
        loads[2].wait()
        for v in range(0, up_tiles, 4):

            def put_upper(i, z, block):
                edge_ref[v + i, z * part_rows : (z + 1) * part_rows] = block

            edges(wu_ref[:, v * 128 : min(v + 4, up_tiles) * 128], 0, upper_levels, put_upper)
        loads[1].wait()

        def put_surface(i, z, block):
            edge_ref[up_tiles, i * part_rows : (i + 1) * part_rows] = block

        edges(ws_ref[...], upper_levels, tok_levels, put_surface)

    def send_edges():
        @pl.when(jnp.logical_not(right_open))
        def _():
            for slot in range(slots):
                for i in range(tiles_of(slot)):
                    edge_copy(first_tile(slot) + i, edge_rows).start()
                if slot == 0:
                    edge_copy(up_tiles, sf_tiles * part_rows).start()

    def take_edge(index, rows):
        edge_copy(index, rows).wait_recv()
        return jnp.dot(
            side_ref[index, 0:rows], spot_ref[...], preferred_element_type=jnp.float32
        )

    def add_rows(channel, h, block):
        at = pl.multiple_of(channel * lat_rows + h * part_rows, 8)
        frame_ref[pl.ds(at, part_rows), :] += block

    def take_upper(t):
        moved = take_edge(t, edge_rows)
        for z in range(upper_levels):
            for h in range(2):
                for l in range(min(2, LEVELS - 2 * z)):
                    lanes = (2 * h + l) * 128
                    block = moved[z * part_rows : (z + 1) * part_rows, lanes : lanes + 128]
                    add_rows(t * LEVELS + 2 * z + l, h, block)

    def take_surface():
        moved = take_edge(up_tiles, sf_tiles * part_rows)
        for i in range(sf_tiles):
            for h in range(2):
                for l in range(2):
                    lanes = (2 * h + l) * 128
                    block = moved[i * part_rows : (i + 1) * part_rows, lanes : lanes + 128]
                    add_rows(VARS_UP * LEVELS + 2 * i + l, h, block)

    def rows_of(window):
        return lax.rem(window + 1, half) == 0

    def copy_of(source, other, rows):
        return pltpu.make_async_remote_copy(
            src_ref=wire_ref.at[other, 0:rows],
            dst_ref=got_ref.at[source, 0:rows],
            send_sem=send_sem.at[other],
            recv_sem=recv_sem.at[source],
            device_id={"win": other},
            device_id_type=pl.DeviceIdType.MESH,
        )

    def either(is_open, run):
        @pl.when(is_open)
        def _():
            run(pad_rows)

        @pl.when(jnp.logical_not(is_open))
        def _():
            run(main_rows)

    def pack_into(ref, index, other):
        start = other * own_rows // PATCH
        main = frame_ref[pl.ds(start, main_rows), :]
        tail = frame_ref[pl.ds(start + main_rows, tail_rows), :]
        parts = [pltpu.roll(tail, shift, 1) for shift in TO_SPARE]
        if main_rows > 3 * tail_rows:
            parts.append(main[3 * tail_rows :])
        kept = own_lanes(main_rows) | right_open
        ref[index, 0:main_rows] = jnp.where(kept, main, jnp.concatenate(parts, axis=0)).astype(
            jnp.bfloat16
        )
        ref[index, main_rows:pad_rows] = tail.astype(jnp.bfloat16)

    def deliver(slot):
        begin, count, more, extra = (
            jnp.where(low, a, b) for a, b in zip(low_plan[slot], high_plan[slot])
        )
        total = count + extra

        def owner(i):
            i = lax.rem(i + me, jnp.maximum(total, 1))
            return jnp.where(i < count, begin + i, more + i - count)

        def send(i, carry):
            one, two = owner(2 * i), owner(jnp.minimum(2 * i + 1, total - 1))
            pack_into(wire_ref, one, one)
            pack_into(wire_ref, two, two)

            @pl.when(one != me)
            def _():
                either(right_open, lambda rows: copy_of(me, one, rows).start())

            @pl.when((two != me) & (2 * i + 1 < total))
            def _():
                either(right_open, lambda rows: copy_of(me, two, rows).start())

            return carry

        lax.fori_loop(0, (total + 1) // 2, send, 0)

    slots = -(-up_tiles // 2)
    tiles = image_ref.shape[1]
    lons = tiles * 128
    groups = windows // GROUP
    pitch = lons // windows
    row = iota((128, GROUP * 128), 0)
    col = iota((128, GROUP * 128), 1)
    row_q, row_column = place_of(row)
    target = row // 64 * 512 + row_q * 128 + row_column

    def fill(i, carry):
        hit = (col == target + i * pitch) & ((row_column < 12) | (i == GROUP - 1))
        place_ref[pl.ds(pl.multiple_of(i * 128, 128), 128), :] = one_hot(hit)
        return carry

    lax.fori_loop(0, GROUP, fill, 0)
    image_ref[...] = jnp.zeros(image_ref.shape, jnp.float32)
    frame_ref[...] = jnp.zeros(frame_ref.shape, jnp.float32)
    make_edges()
    pl.semaphore_wait(barrier, windows - 1)
    send_edges()
    for slot in range(slots):
        t, count = first_tile(slot), tiles_of(slot)
        spread(wu_ref[:, pl.ds(pl.multiple_of(t * 128, 128), count * 128)])
        if slot == 0:
            loads[3].wait()
        multiply(0, upper_levels)
        for z in range(upper_levels):
            merge(
                z,
                [
                    (t + i) * LEVELS + 2 * z + l if 2 * z + l < LEVELS else None
                    for i in range(count)
                    for l in range(2)
                ],
            )
        if slot == 1:
            spread(ws_ref[...])
            multiply(upper_levels, tok_levels)
            merge(0, [VARS_UP * LEVELS + v for v in range(VARS_SF)])

        @pl.when(jnp.logical_not(left_open))
        def _():
            for i in range(count):
                take_upper(t + i)
            if slot == 1:
                take_surface()

        deliver(slot)
    pack_into(got_ref, me, me)

    def unpack(source, may_be_open):
        main = got_ref[source, 0:main_rows]
        tail = jnp.zeros((tail_rows, 128), jnp.float32)
        for c in range(3):
            part = got_ref[source, c * tail_rows : (c + 1) * tail_rows].astype(jnp.float32)
            part = pltpu.roll(part, 128 - TO_SPARE[c], 1)
            tail = jnp.where(chunk_lanes(tail_rows, c), part, tail)
        if may_be_open:
            is_open = rows_of(source)
            raw = got_ref[source, main_rows:pad_rows].astype(jnp.float32)
            tail = jnp.where(is_open, raw, tail)
            wide = jnp.where(own_lanes(main_rows) | is_open, main.astype(jnp.float32), 0.0)
            main = wide.astype(jnp.bfloat16)
        return jnp.concatenate([main, tail.astype(jnp.bfloat16)], axis=0)

    def gather(k, carry):
        g = partner(me // GROUP, k, groups)

        def wait_one(i, inner):
            source = g * GROUP + i

            @pl.when(source != me)
            def _():
                either(rows_of(source), lambda rows: copy_of(source, source, rows).wait_recv())

            return inner

        lax.fori_loop(0, GROUP, wait_one, 0)
        stacked = jnp.concatenate(
            [unpack(g * GROUP + i, i == GROUP - 1) for i in range(GROUP)], axis=1
        )
        moved = jnp.dot(stacked, place_ref[...], preferred_element_type=jnp.float32)
        start = g * (GROUP * pitch) + (lons - PATCH // 2)
        shift = lax.rem(start, 128)
        tile = lax.rem(start // 128, tiles)
        after = lax.rem(tile + 1, tiles)
        first_part = lane_of_pad >= shift
        for m in range(members):
            for q in range(PATCH):
                at = (m * PATCH + q) * 128
                value = pltpu.roll(moved[:, at : at + 128], shift, 1)
                rows = pl.ds(q, pad_rows, stride=PATCH)
                image_ref[m, tile, rows, :] += jnp.where(first_part, value, 0.0)
                image_ref[m, after, rows, :] += jnp.where(first_part, 0.0, value)
        return carry

    lane_of_pad = lax.broadcasted_iota(jnp.int32, (pad_rows, 128), 1)
    lax.fori_loop(0, groups, gather, 0)

    begin = 0 if own_rows % PATCH == 0 else lax.rem(me * own_rows, PATCH)
    for m in range(members):
        for tile in range(tiles):
            rows = image_ref[m, tile, pl.ds(begin, own_rows), :]
            out_ref[m, :, tile * 128 : (tile + 1) * 128] = rows.astype(jnp.bfloat16)

    def sent(r, carry):
        other = partner(me, r, windows)
        either(right_open, lambda rows: copy_of(me, other, rows).wait_send())
        return carry

    lax.fori_loop(1, windows, sent, 0)

    @pl.when(jnp.logical_not(right_open))
    def _():
        for index in range(up_tiles):
            edge_copy(index, edge_rows).wait_send()
        edge_copy(up_tiles, sf_tiles * part_rows).wait_send()


def rows_for(longest):
    main = 16
    while True:
        tail = max(16, -(-(longest - main) // 16) * 16)
        if 3 * tail <= main:
            return main, tail
        main += 16


def plan_of(spans, lat_rows, tiles):
    owners, depth = len(spans), LEVELS * lat_rows
    surface, slots = tiles * depth, -(-tiles // 2)
    inner = [o for o in range(owners) if spans[o][1] <= surface]
    low, high = [], []
    done_low, done_high = inner[-1] + 1, 0
    for slot in range(slots):
        floor = max(tiles - 2 * (slot + 1), 0) * depth
        begin = min(o for o in range(owners) if spans[o][0] >= floor)
        begin = min(begin, done_low)
        extra = owners - inner[-1] - 1 if slot == 1 else 0
        low.append((begin, done_low - begin, inner[-1] + 1, extra))
        done_low = begin
        ready = sum(1 for lo, hi in spans if hi <= min(2 * (slot + 1), tiles) * depth)
        ready = owners if slot == slots - 1 else ready
        high.append((done_high, ready - done_high, 0, 0))
        done_high = ready
    return low, high


def body(tokens, w_upper, w_surface, bias):
    members, tok_levels, lat_rows, lon_cols, width = tokens.shape
    windows = lax.axis_size("win")
    own_rows = CHANNELS * lat_rows * PATCH // windows
    lons = windows * lon_cols * PATCH
    spans = spans_of(windows, own_rows)
    main_rows, tail_rows = rows_for(max(hi - lo for lo, hi in spans))
    pad_rows = main_rows + tail_rows
    frame_rows = -(-(spans[-1][0] + pad_rows) // 8) * 8
    low_plan, high_plan = plan_of(spans, lat_rows, w_upper.shape[1] // 128)
    edges = w_upper.shape[1] // 128 + 1
    bf16, f32 = jnp.bfloat16, jnp.float32
    by_lon = jnp.transpose(tokens, (0, 1, 3, 2, 4))
    return pl.pallas_call(
        functools.partial(kernel, (own_rows, main_rows, low_plan, high_plan)),
        out_shape=pltpu.VMEM((members, own_rows, lons), bf16),
        in_specs=[pl.BlockSpec(memory_space=pltpu.HBM)] * 3
        + [pl.BlockSpec(memory_space=pltpu.SMEM)],
        out_specs=pl.BlockSpec(memory_space=pltpu.VMEM),
        scratch_shapes=[
            pltpu.VMEM(by_lon.shape, bf16),
            pltpu.VMEM(w_upper.shape, bf16),
            pltpu.VMEM(w_surface.shape, bf16),
            pltpu.VMEM((2, 2 * width, 256), bf16),
            pltpu.VMEM((members, 2, (tok_levels - 1) * lat_rows, 256), f32),
            pltpu.VMEM((frame_rows, 128), f32),
            pltpu.VMEM((windows, pad_rows, 128), bf16),
            pltpu.VMEM((windows, pad_rows, 128), bf16),
            pltpu.VMEM((edges, (tok_levels - 1) * lat_rows // 2, 128), bf16),
            pltpu.VMEM((edges, (tok_levels - 1) * lat_rows // 2, 128), bf16),
            pltpu.VMEM((128, 4 * 128), bf16),
            pltpu.VMEM((256, 1024), bf16),
            pltpu.VMEM((512, 256), bf16),
            pltpu.VMEM((GROUP * 128, GROUP * 128), bf16),
            pltpu.VMEM((members, lons // 128, pad_rows * PATCH, 128), f32),
            pltpu.SemaphoreType.DMA((4,)),
            pltpu.SemaphoreType.DMA((windows,)),
            pltpu.SemaphoreType.DMA((windows,)),
            pltpu.SemaphoreType.DMA((2, edges)),
        ],
        compiler_params=pltpu.CompilerParams(
            collective_id=0, has_side_effects=True, vmem_limit_bytes=65 * 1000 * 1000
        ),
    )(by_lon, w_upper, w_surface, bias)


def solution(mesh):
    placed = (P("grp", None, None, "win", None), P(), P(), P())
    return jax.shard_map(
        body, mesh=mesh, in_specs=placed, out_specs=P("grp", "win", None), check_vma=False
    )
```

time: 37.2 us -> 33.7 us (0.906)
  Pallas kernels: 36.1 us -> 32.6 us
    pallas_call x1, Pallas kernels: 36.1 us -> 32.6 us  [body(): pl.pallas_call(functools.partial(kernel, (own_rows, main_rows, low_plan,...]
where the time goes in v3:
time: 33.7 us; the launch traced here: 33.5 us
  Pallas kernels  32.6 us (97%)
  local copies, waits for them, and re-layouts  0.9 us (3%)
    pallas_call x1, Pallas kernels, body(): pl.pallas_call(functools.partial(kernel, (own_rows, main_rows, low_plan,...  32.6 us
    unnamed x1, local copies, waits for them, and re-layouts  0.9 us

profile of v3, /device:TPU:0, one launch (start us, length us, event | category | flops | bytes accessed | tf_op | source)
XLA Modules:
  0.0 33.5 jit_solution(7273567277773364801)
XLA Ops:
  0.0 32.6 %shard_map.46 = bf16[2,552,384]{2,1,0:T(8,128)(2,1)S(1)} custom-call(bf16[2,8,3,64,384]{4,3,2,1,0:T(8,128)(2,1)} %bitcast.1, bf16[384,640]{1,0:T(8,128)(2,1)} %wu_hbm.1, bf16[384,256]{1,0:T(8,128)(2,1)} %ws_hbm.1, f32[69]{0:T(128)} %bias_ref.1), custom_call_target="tpu_custom_call" | custom-call | tf_op jit(solution)/shard_map/pallas_call | solution.py:494
  32.6 0.9 %copy.6 = bf16[2,552,384]{2,1,0:T(8,128)(2,1)} copy(bf16[2,552,384]{2,1,0:T(8,128)(2,1)S(1)} %shard_map.46) | data formatting | bytes 1695744

commit v4 on v3

--- a/solution.py
+++ b/solution.py
@@ -35,7 +35,7 @@
 def kernel(
     plan, tok_hbm, wu_hbm, ws_hbm, bias_ref, out_ref,
     tok_ref, wu_ref, ws_ref, wb_ref, proj_ref, frame_ref, wire_ref, got_ref, edge_ref, side_ref, spot_ref,
-    sel_ref, pick_ref,    place_ref, image_ref, load_sem, send_sem, recv_sem, edge_sem,
+    sel_ref, pick_ref,    place_ref, image_ref, wide_ref, load_sem, send_sem, recv_sem, edge_sem,
 ):
     members, tok_levels, lon_cols, lat_rows, width = tok_ref.shape
     windows, pad_rows, _ = wire_ref.shape
@@ -44,8 +44,7 @@
     up_tiles = wu_ref.shape[1] // 128
     sf_tiles = ws_ref.shape[1] // 128
     me = lax.axis_index("win")
-    own_rows, main_rows, low_plan, high_plan = plan
-    tail_rows = pad_rows - main_rows
+    own_rows, main_rows, extra_rows, sends = plan
 
     last = lon_cols - 1
     loads = [
@@ -176,7 +175,8 @@
     low = me < half
 
     def first_tile(slot):
-        return jnp.where(low, max(up_tiles - 2 * (slot + 1), 0), 2 * slot)
+        low_tiles, high_tiles = tile_order(up_tiles)
+        return jnp.where(low, low_tiles[slot], high_tiles[slot])
 
     def tiles_of(slot):
         return min(2, up_tiles - 2 * slot)
@@ -215,15 +215,14 @@
                 put_edge(i, z, block.astype(jnp.bfloat16))
 
     def make_edges():
-        loads[0].wait()
-        loads[2].wait()
+        for load in loads[:3]:
+            load.wait()
         for v in range(0, up_tiles, 4):
 
             def put_upper(i, z, block):
                 edge_ref[v + i, z * part_rows : (z + 1) * part_rows] = block
 
             edges(wu_ref[:, v * 128 : min(v + 4, up_tiles) * 128], 0, upper_levels, put_upper)
-        loads[1].wait()
 
         def put_surface(i, z, block):
             edge_ref[up_tiles, i * part_rows : (i + 1) * part_rows] = block
@@ -236,7 +235,7 @@
             for slot in range(slots):
                 for i in range(tiles_of(slot)):
                     edge_copy(first_tile(slot) + i, edge_rows).start()
-                if slot == 0:
+                if slot == slots - 1:
                     edge_copy(up_tiles, sf_tiles * part_rows).start()
 
     def take_edge(index, rows):
@@ -292,50 +291,60 @@
     def pack_into(ref, index, other):
         start = other * own_rows // PATCH
         main = frame_ref[pl.ds(start, main_rows), :]
-        tail = frame_ref[pl.ds(start + main_rows, tail_rows), :]
-        parts = [pltpu.roll(tail, shift, 1) for shift in TO_SPARE]
-        if main_rows > 3 * tail_rows:
-            parts.append(main[3 * tail_rows :])
+        tail = frame_ref[pl.ds(start + main_rows, pad_rows - main_rows), :]
+        chunks = []
+        for c in range(3):
+            first = c * extra_rows // 8 * 8
+            end = min(-(-(c + 1) * extra_rows // 8) * 8, main_rows) if c < 2 else main_rows
+            rows = frame_ref[pl.ds(start + main_rows - c * extra_rows + first, end - first), :]
+            chunks.append((first, pltpu.roll(rows, TO_SPARE[c], 1)))
+        line_of_8 = iota((8, 128), 0)
+        spare = []
+        for at in range(0, main_rows, 8):
+            block = None
+            for c, (first, rows) in enumerate(chunks):
+                if first <= at < first + rows.shape[0]:
+                    part = rows[at - first : at - first + 8]
+                    begins = line_of_8 >= c * extra_rows - at
+                    block = part if block is None else jnp.where(begins, part, block)
+            spare.append(block)
         kept = own_lanes(main_rows) | right_open
-        ref[index, 0:main_rows] = jnp.where(kept, main, jnp.concatenate(parts, axis=0)).astype(
-            jnp.bfloat16
-        )
-        ref[index, main_rows:pad_rows] = tail.astype(jnp.bfloat16)
-
-    def deliver(slot):
-        begin, count, more, extra = (
-            jnp.where(low, a, b) for a, b in zip(low_plan[slot], high_plan[slot])
-        )
-        total = count + extra
-
-        def owner(i):
-            i = lax.rem(i + me, jnp.maximum(total, 1))
-            return jnp.where(i < count, begin + i, more + i - count)
+        main = jnp.where(kept, main, jnp.concatenate(spare, axis=0))
+        ref[index] = jnp.concatenate([main, tail], axis=0).astype(jnp.bfloat16)
+
+    pair_of_me = me // 2
+
+    def serve(low_range, high_range):
+        begin, end = (jnp.where(low, a, b) for a, b in zip(low_range, high_range))
+        first_pair = begin // 2
+        pairs = (end + 1) // 2 - first_pair
 
         def send(i, carry):
-            one, two = owner(2 * i), owner(jnp.minimum(2 * i + 1, total - 1))
-            pack_into(wire_ref, one, one)
-            pack_into(wire_ref, two, two)
-
-            @pl.when(one != me)
+            pair = first_pair + lax.rem(i + pair_of_me, jnp.maximum(pairs, 1))
+            one, two = 2 * pair, 2 * pair + 1
+            first, second = jnp.maximum(one, begin), jnp.minimum(two, end - 1)
+            pack_into(wire_ref, first, first)
+            pack_into(wire_ref, second, second)
+
+            @pl.when((one != me) & (one >= begin))
             def _():
                 either(right_open, lambda rows: copy_of(me, one, rows).start())
 
-            @pl.when((two != me) & (2 * i + 1 < total))
+            @pl.when((two != me) & (two < end))
             def _():
                 either(right_open, lambda rows: copy_of(me, two, rows).start())
 
             return carry
 
-        lax.fori_loop(0, (total + 1) // 2, send, 0)
+        lax.fori_loop(0, pairs, send, 0)
 
     slots = -(-up_tiles // 2)
     tiles = image_ref.shape[1]
     lons = tiles * 128
     groups = windows // GROUP
     pitch = lons // windows
-    row = iota((128, GROUP * 128), 0)
-    col = iota((128, GROUP * 128), 1)
+    row = iota((128, place_ref.shape[1]), 0)
+    col = iota(row.shape, 1)
     row_q, row_column = place_of(row)
     target = row // 64 * 512 + row_q * 128 + row_column
 
@@ -347,14 +356,23 @@
     lax.fori_loop(0, GROUP, fill, 0)
     image_ref[...] = jnp.zeros(image_ref.shape, jnp.float32)
     frame_ref[...] = jnp.zeros(frame_ref.shape, jnp.float32)
+    def spread_upper(slot):
+        t, count = first_tile(slot), tiles_of(slot)
+        spread(wu_ref[:, pl.ds(pl.multiple_of(t * 128, 128), count * 128)])
+
+    def meet():
+        pl.semaphore_wait(barrier, windows - 1)
+        send_edges()
+
     make_edges()
-    pl.semaphore_wait(barrier, windows - 1)
-    send_edges()
+    spread_upper(0)
+    early = me < windows // 4
+    pl.when(jnp.logical_not(early))(meet)
+    loads[3].wait()
     for slot in range(slots):
         t, count = first_tile(slot), tiles_of(slot)
-        spread(wu_ref[:, pl.ds(pl.multiple_of(t * 128, 128), count * 128)])
-        if slot == 0:
-            loads[3].wait()
+        if slot > 0:
+            spread_upper(slot)
         multiply(0, upper_levels)
         for z in range(upper_levels):
             merge(
@@ -365,7 +383,9 @@
                     for l in range(2)
                 ],
             )
-        if slot == 1:
+        if slot == 0:
+            pl.when(early)(meet)
+        if slot == slots - 1:
             spread(ws_ref[...])
             multiply(upper_levels, tok_levels)
             merge(0, [VARS_UP * LEVELS + v for v in range(VARS_SF)])
@@ -374,26 +394,28 @@
         def _():
             for i in range(count):
                 take_upper(t + i)
-            if slot == 1:
+            if slot == slots - 1:
                 take_surface()
 
-        deliver(slot)
+        for low_range, high_range in sends[slot]:
+            serve(low_range, high_range)
     pack_into(got_ref, me, me)
 
-    def unpack(source, may_be_open):
-        main = got_ref[source, 0:main_rows]
-        tail = jnp.zeros((tail_rows, 128), jnp.float32)
+    def unpack(i, source):
+        rows = got_ref[source].astype(jnp.float32)
+        wide_ref[i] = rows
+        main, raw = rows[:main_rows], rows[main_rows:]
+        count = pad_rows - main_rows
+        tail = jnp.zeros((count, 128), jnp.float32)
         for c in range(3):
-            part = got_ref[source, c * tail_rows : (c + 1) * tail_rows].astype(jnp.float32)
+            part = wide_ref[i, c * extra_rows : c * extra_rows + count]
             part = pltpu.roll(part, 128 - TO_SPARE[c], 1)
-            tail = jnp.where(chunk_lanes(tail_rows, c), part, tail)
-        if may_be_open:
+            tail = jnp.where(chunk_lanes(count, c), part, tail)
+        if i == GROUP - 1:
             is_open = rows_of(source)
-            raw = got_ref[source, main_rows:pad_rows].astype(jnp.float32)
             tail = jnp.where(is_open, raw, tail)
-            wide = jnp.where(own_lanes(main_rows) | is_open, main.astype(jnp.float32), 0.0)
-            main = wide.astype(jnp.bfloat16)
-        return jnp.concatenate([main, tail.astype(jnp.bfloat16)], axis=0)
+            main = jnp.where(own_lanes(main_rows) | is_open, main, 0.0)
+        return jnp.concatenate([main, tail], axis=0).astype(jnp.bfloat16)
 
     def gather(k, carry):
         g = partner(me // GROUP, k, groups)
@@ -409,7 +431,7 @@
 
         lax.fori_loop(0, GROUP, wait_one, 0)
         stacked = jnp.concatenate(
-            [unpack(g * GROUP + i, i == GROUP - 1) for i in range(GROUP)], axis=1
+            [unpack(i, g * GROUP + i) for i in range(GROUP)], axis=1
         )
         moved = jnp.dot(stacked, place_ref[...], preferred_element_type=jnp.float32)
         start = g * (GROUP * pitch) + (lons - PATCH // 2)
@@ -449,33 +471,45 @@
         edge_copy(up_tiles, sf_tiles * part_rows).wait_send()
 
 
-def rows_for(longest):
-    main = 16
-    while True:
-        tail = max(16, -(-(longest - main) // 16) * 16)
-        if 3 * tail <= main:
-            return main, tail
-        main += 16
+def tile_order(tiles):
+    return (tiles - 2, 0, 2), (0, tiles - 2, 2)
+
+
+def ranges_of(owners):
+    ranges = []
+    for o in owners:
+        if ranges and ranges[-1][1] == o:
+            ranges[-1][1] = o + 1
+        else:
+            ranges.append([o, o + 1])
+    return ranges
 
 
 def plan_of(spans, lat_rows, tiles):
     owners, depth = len(spans), LEVELS * lat_rows
-    surface, slots = tiles * depth, -(-tiles // 2)
-    inner = [o for o in range(owners) if spans[o][1] <= surface]
-    low, high = [], []
-    done_low, done_high = inner[-1] + 1, 0
-    for slot in range(slots):
-        floor = max(tiles - 2 * (slot + 1), 0) * depth
-        begin = min(o for o in range(owners) if spans[o][0] >= floor)
-        begin = min(begin, done_low)
-        extra = owners - inner[-1] - 1 if slot == 1 else 0
-        low.append((begin, done_low - begin, inner[-1] + 1, extra))
-        done_low = begin
-        ready = sum(1 for lo, hi in spans if hi <= min(2 * (slot + 1), tiles) * depth)
-        ready = owners if slot == slots - 1 else ready
-        high.append((done_high, ready - done_high, 0, 0))
-        done_high = ready
-    return low, high
+    half, slots = owners // 2, -(-tiles // 2)
+    sides = []
+    for first, own in zip(tile_order(tiles), (range(half), range(half, owners))):
+        done, sent, fresh = set(), set(), []
+        for slot in range(slots):
+            for t in range(first[slot], first[slot] + min(2, tiles - 2 * slot)):
+                done.update(range(t * depth, (t + 1) * depth))
+            if slot == slots - 1:
+                done.update(range(tiles * depth, spans[-1][1]))
+            new = [
+                o for o in range(owners) if o not in sent and done.issuperset(range(*spans[o]))
+            ]
+            sent.update(new)
+            fresh.append(([o for o in new if o in own], [o for o in new if o not in own]))
+        sides.append(fresh)
+
+    def both(slot, far):
+        low, high = (ranges_of(side[slot][far]) for side in sides)
+        count = max(len(low), len(high))
+        low, high = (x + [[0, 0]] * (count - len(x)) for x in (low, high))
+        return list(zip(low, high))
+
+    return [both(0, 1) + both(0, 0)] + [both(slot, 0) + both(slot, 1) for slot in range(1, slots)]
 
 
 def body(tokens, w_upper, w_surface, bias):
@@ -484,15 +518,17 @@
     own_rows = CHANNELS * lat_rows * PATCH // windows
     lons = windows * lon_cols * PATCH
     spans = spans_of(windows, own_rows)
-    main_rows, tail_rows = rows_for(max(hi - lo for lo, hi in spans))
-    pad_rows = main_rows + tail_rows
+    longest = max(hi - lo for lo, hi in spans)
+    main_rows = -(-3 * longest // 32) * 8
+    extra_rows = max(longest - main_rows, 1)
+    pad_rows = -(-longest // 16) * 16
     frame_rows = -(-(spans[-1][0] + pad_rows) // 8) * 8
-    low_plan, high_plan = plan_of(spans, lat_rows, w_upper.shape[1] // 128)
+    sends = plan_of(spans, lat_rows, w_upper.shape[1] // 128)
     edges = w_upper.shape[1] // 128 + 1
     bf16, f32 = jnp.bfloat16, jnp.float32
     by_lon = jnp.transpose(tokens, (0, 1, 3, 2, 4))
     return pl.pallas_call(
-        functools.partial(kernel, (own_rows, main_rows, low_plan, high_plan)),
+        functools.partial(kernel, (own_rows, main_rows, extra_rows, sends)),
         out_shape=pltpu.VMEM((members, own_rows, lons), bf16),
         in_specs=[pl.BlockSpec(memory_space=pltpu.HBM)] * 3
         + [pl.BlockSpec(memory_space=pltpu.SMEM)],
@@ -511,8 +547,9 @@
             pltpu.VMEM((128, 4 * 128), bf16),
             pltpu.VMEM((256, 1024), bf16),
             pltpu.VMEM((512, 256), bf16),
-            pltpu.VMEM((GROUP * 128, GROUP * 128), bf16),
+            pltpu.VMEM((GROUP * 128, members * PATCH * 128), bf16),
             pltpu.VMEM((members, lons // 128, pad_rows * PATCH, 128), f32),
+            pltpu.VMEM((GROUP, pad_rows, 128), f32),
             pltpu.SemaphoreType.DMA((4,)),
             pltpu.SemaphoreType.DMA((windows,)),
             pltpu.SemaphoreType.DMA((windows,)),

time: 33.7 us -> 32.5 us (0.964)
  Pallas kernels: 32.6 us -> 31.4 us
    pallas_call x1, Pallas kernels: 32.6 us -> 31.4 us  [body(): pl.pallas_call(functools.partial(kernel, (own_rows, main_rows, extra_rows...]
where the time goes in v4:
time: 32.5 us; the launch traced here: 32.3 us
  Pallas kernels  31.4 us (97%)
  local copies, waits for them, and re-layouts  0.9 us (3%)
    pallas_call x1, Pallas kernels, body(): pl.pallas_call(functools.partial(kernel, (own_rows, main_rows, extra_rows...  31.4 us
    unnamed x1, local copies, waits for them, and re-layouts  0.9 us

profile of v4, /device:TPU:0, one launch (start us, length us, event | category | flops | bytes accessed | tf_op | source)
XLA Modules:
  0.0 32.3 jit_solution(2551855733942990130)
XLA Ops:
  0.0 31.4 %shard_map.46 = bf16[2,552,384]{2,1,0:T(8,128)(2,1)S(1)} custom-call(bf16[2,8,3,64,384]{4,3,2,1,0:T(8,128)(2,1)} %bitcast.1, bf16[384,640]{1,0:T(8,128)(2,1)} %wu_hbm.1, bf16[384,256]{1,0:T(8,128)(2,1)} %ws_hbm.1, f32[69]{0:T(128)} %bias_ref.1), custom_call_target="tpu_custom_call" | custom-call | tf_op jit(solution)/shard_map/pallas_call | solution.py:530
  31.4 0.9 %copy.6 = bf16[2,552,384]{2,1,0:T(8,128)(2,1)} copy(bf16[2,552,384]{2,1,0:T(8,128)(2,1)S(1)} %shard_map.46) | data formatting | bytes 1695744

commit v5 on v4

--- a/solution.py
+++ b/solution.py
@@ -314,25 +314,29 @@
 
     pair_of_me = me // 2
 
-    def serve(low_range, high_range):
+    def serve(low_range, high_range, near):
         begin, end = (jnp.where(low, a, b) for a, b in zip(low_range, high_range))
         first_pair = begin // 2
         pairs = (end + 1) // 2 - first_pair
 
         def send(i, carry):
             pair = first_pair + lax.rem(i + pair_of_me, jnp.maximum(pairs, 1))
-            one, two = 2 * pair, 2 * pair + 1
-            first, second = jnp.maximum(one, begin), jnp.minimum(two, end - 1)
-            pack_into(wire_ref, first, first)
-            pack_into(wire_ref, second, second)
-
-            @pl.when((one != me) & (one >= begin))
+            wanted = True if near is None else (lax.rem(pair // 2, 2) == lax.rem(pair_of_me // 2, 2)) == near
+
+            @pl.when(wanted)
             def _():
-                either(right_open, lambda rows: copy_of(me, one, rows).start())
-
-            @pl.when((two != me) & (two < end))
-            def _():
-                either(right_open, lambda rows: copy_of(me, two, rows).start())
+                one, two = 2 * pair, 2 * pair + 1
+                first, second = jnp.maximum(one, begin), jnp.minimum(two, end - 1)
+                pack_into(wire_ref, first, first)
+                pack_into(wire_ref, second, second)
+
+                @pl.when((one != me) & (one >= begin))
+                def _():
+                    either(right_open, lambda rows: copy_of(me, one, rows).start())
+
+                @pl.when((two != me) & (two < end))
+                def _():
+                    either(right_open, lambda rows: copy_of(me, two, rows).start())
 
             return carry
 
@@ -364,9 +368,21 @@
         pl.semaphore_wait(barrier, windows - 1)
         send_edges()
 
+    def settle(slot):
+        @pl.when(jnp.logical_not(left_open))
+        def _():
+            for i in range(tiles_of(slot)):
+                take_upper(first_tile(slot) + i)
+            if slot == slots - 1:
+                take_surface()
+
+        for low_range, high_range, near in sends[slot]:
+            serve(low_range, high_range, near)
+
     make_edges()
     spread_upper(0)
     early = me < windows // 4
+    earliest = me < windows // 16
     pl.when(jnp.logical_not(early))(meet)
     loads[3].wait()
     for slot in range(slots):
@@ -383,22 +399,23 @@
                     for l in range(2)
                 ],
             )
-        if slot == 0:
-            pl.when(early)(meet)
         if slot == slots - 1:
             spread(ws_ref[...])
             multiply(upper_levels, tok_levels)
             merge(0, [VARS_UP * LEVELS + v for v in range(VARS_SF)])
 
-        @pl.when(jnp.logical_not(left_open))
-        def _():
-            for i in range(count):
-                take_upper(t + i)
-            if slot == slots - 1:
-                take_surface()
-
-        for low_range, high_range in sends[slot]:
-            serve(low_range, high_range)
+        if slot == 0:
+            pl.when(early & jnp.logical_not(earliest))(meet)
+            pl.when(jnp.logical_not(earliest))(functools.partial(settle, 0))
+        else:
+            if slot == 1:
+
+                @pl.when(earliest)
+                def _():
+                    meet()
+                    settle(0)
+
+            settle(slot)
     pack_into(got_ref, me, me)
 
     def unpack(i, source):
@@ -503,13 +520,19 @@
             fresh.append(([o for o in new if o in own], [o for o in new if o not in own]))
         sides.append(fresh)
 
-    def both(slot, far):
+    def both(slot, far, near):
         low, high = (ranges_of(side[slot][far]) for side in sides)
         count = max(len(low), len(high))
         low, high = (x + [[0, 0]] * (count - len(x)) for x in (low, high))
-        return list(zip(low, high))
-
-    return [both(0, 1) + both(0, 0)] + [both(slot, 0) + both(slot, 1) for slot in range(1, slots)]
+        return [(a, b, near) for a, b in zip(low, high)]
+
+    sends = [both(0, 1, True)]
+    for slot in range(1, slots):
+        now = both(0, 0, None) if slot == 1 else []
+        now += both(slot, 0, None)
+        now += both(0, 1, False) if slot == 1 else []
+        sends.append(now + both(slot, 1, None))
+    return sends
 
 
 def body(tokens, w_upper, w_surface, bias):

time: 32.5 us -> 31.9 us (0.982)
  Pallas kernels: 31.4 us -> 30.7 us
    pallas_call x1, Pallas kernels: 31.4 us -> 30.7 us  [body(): pl.pallas_call(functools.partial(kernel, (own_rows, main_rows, extra_rows...]
where the time goes in v5:
time: 31.9 us; the launch traced here: 31.6 us
  Pallas kernels  30.7 us (96%)
  local copies, waits for them, and re-layouts  0.9 us (3%)
    pallas_call x1, Pallas kernels, body(): pl.pallas_call(functools.partial(kernel, (own_rows, main_rows, extra_rows...  30.7 us
    unnamed x1, local copies, waits for them, and re-layouts  0.9 us

profile of v5, /device:TPU:0, one launch (start us, length us, event | category | flops | bytes accessed | tf_op | source)
XLA Modules:
  0.0 31.6 jit_solution(4131314887264125055)
XLA Ops:
  0.0 30.7 %shard_map.46 = bf16[2,552,384]{2,1,0:T(8,128)(2,1)S(1)} custom-call(bf16[2,8,3,64,384]{4,3,2,1,0:T(8,128)(2,1)} %bitcast.1, bf16[384,640]{1,0:T(8,128)(2,1)} %wu_hbm.1, bf16[384,256]{1,0:T(8,128)(2,1)} %ws_hbm.1, f32[69]{0:T(128)} %bias_ref.1), custom_call_target="tpu_custom_call" | custom-call | tf_op jit(solution)/shard_map/pallas_call | solution.py:553
  30.7 0.9 %copy.6 = bf16[2,552,384]{2,1,0:T(8,128)(2,1)} copy(bf16[2,552,384]{2,1,0:T(8,128)(2,1)S(1)} %shard_map.46) | data formatting | bytes 1695744

commit v6 on v5

--- a/solution.py
+++ b/solution.py
@@ -62,7 +62,7 @@
 
     def greet(r, carry):
         pl.semaphore_signal(
-            barrier, inc=1, device_id={"win": partner(me, r, windows)},
+            barrier, inc=1, device_id={"win": partner(me, windows - r, windows)},
             device_id_type=pl.DeviceIdType.MESH,
         )
         return carry
@@ -529,8 +529,8 @@
     sends = [both(0, 1, True)]
     for slot in range(1, slots):
         now = both(0, 0, None) if slot == 1 else []
+        now += both(0, 1, False) if slot == 1 else []
         now += both(slot, 0, None)
-        now += both(0, 1, False) if slot == 1 else []
         sends.append(now + both(slot, 1, None))
     return sends
 

time: 31.9 us -> 31.8 us (level)
  no operation moved by 1% of the time
where the time goes in v6:
time: 31.8 us; the launch traced here: 31.6 us
  Pallas kernels  30.7 us (97%)
  local copies, waits for them, and re-layouts  0.9 us (3%)
    pallas_call x1, Pallas kernels, body(): pl.pallas_call(functools.partial(kernel, (own_rows, main_rows, extra_rows...  30.7 us
    unnamed x1, local copies, waits for them, and re-layouts  0.9 us

profile of v6, /device:TPU:0, one launch (start us, length us, event | category | flops | bytes accessed | tf_op | source)
XLA Modules:
  0.0 31.6 jit_solution(10324287359230219345)
XLA Ops:
  0.0 30.7 %shard_map.46 = bf16[2,552,384]{2,1,0:T(8,128)(2,1)S(1)} custom-call(bf16[2,8,3,64,384]{4,3,2,1,0:T(8,128)(2,1)} %bitcast.1, bf16[384,640]{1,0:T(8,128)(2,1)} %wu_hbm.1, bf16[384,256]{1,0:T(8,128)(2,1)} %ws_hbm.1, f32[69]{0:T(128)} %bias_ref.1), custom_call_target="tpu_custom_call" | custom-call | tf_op jit(solution)/shard_map/pallas_call | solution.py:553
  30.7 0.9 %copy.6 = bf16[2,552,384]{2,1,0:T(8,128)(2,1)} copy(bf16[2,552,384]{2,1,0:T(8,128)(2,1)S(1)} %shard_map.46) | data formatting | bytes 1695744

commit v7 on v6

--- a/solution.py
+++ b/solution.py
@@ -434,8 +434,10 @@
             main = jnp.where(own_lanes(main_rows) | is_open, main, 0.0)
         return jnp.concatenate([main, tail], axis=0).astype(jnp.bfloat16)
 
+    outer = (me < windows // 4) | (me >= windows - windows // 4)
+
     def gather(k, carry):
-        g = partner(me // GROUP, k, groups)
+        g = partner(me // GROUP, jnp.where(outer & (k >= 2), groups + 1 - k, k), groups)
 
         def wait_one(i, inner):
             source = g * GROUP + i

time: 31.8 us -> 31.8 us (level)
  no operation moved by 1% of the time
where the time goes in v7:
time: 31.8 us; the launch traced here: 31.6 us
  Pallas kernels  30.7 us (97%)
  local copies, waits for them, and re-layouts  0.9 us (3%)
    pallas_call x1, Pallas kernels, body(): pl.pallas_call(functools.partial(kernel, (own_rows, main_rows, extra_rows...  30.7 us
    unnamed x1, local copies, waits for them, and re-layouts  0.9 us

profile of v7, /device:TPU:0, one launch (start us, length us, event | category | flops | bytes accessed | tf_op | source)
XLA Modules:
  0.0 31.6 jit_solution(13458627625331512064)
XLA Ops:
  0.0 30.7 %shard_map.46 = bf16[2,552,384]{2,1,0:T(8,128)(2,1)S(1)} custom-call(bf16[2,8,3,64,384]{4,3,2,1,0:T(8,128)(2,1)} %bitcast.1, bf16[384,640]{1,0:T(8,128)(2,1)} %wu_hbm.1, bf16[384,256]{1,0:T(8,128)(2,1)} %ws_hbm.1, f32[69]{0:T(128)} %bias_ref.1), custom_call_target="tpu_custom_call" | custom-call | tf_op jit(solution)/shard_map/pallas_call | solution.py:555
  30.7 0.9 %copy.6 = bf16[2,552,384]{2,1,0:T(8,128)(2,1)} copy(bf16[2,552,384]{2,1,0:T(8,128)(2,1)S(1)} %shard_map.46) | data formatting | bytes 1695744
